TPU v7x, 32 devices: a whole 2x2x4 slice. The times are simulated.
32 devices in a mesh: seq: 8 (over z, y), tensor: 4 (over x, core).
Axes of the slice: x: 2, y: 2, z: 4, core: 2. Of those that a mesh axis runs over, the one named last changes fastest.
Arguments:
- hidden_in: bfloat16 [1024, 8192], P('seq', 'tensor'), may hold values from -6 to 6
- grad_out: bfloat16 [1024, 8192], P('seq', 'tensor'), may hold values from -6 to 6
- slot_tokens: int32 [128], P('seq'), may hold values from 0 to 127, as said below
- live_counts: int32 [8], P('seq'), may hold values from 5 to 16, as said below
- norm_gain: float32 [8192], P('tensor'), may hold values from 0.5 to 1.5
- router_weight: float32 [8192], P('tensor'), may hold values from -0.0625 to 0.0625
- gate_weight: bfloat16 [8192, 24576], P('tensor', 'seq'), may hold values from -0.0625 to 0.0625
- up_weight: bfloat16 [8192, 24576], P('tensor', 'seq'), may hold values from -0.0625 to 0.0625
- down_weight: bfloat16 [24576, 8192], P('seq', 'tensor'), may hold values from -0.0390625 to 0.0390625
Outputs:
- grad_in: bfloat16 [1024, 8192], P('seq', 'tensor')
- grad_gate: bfloat16 [8192, 24576], P('tensor', 'seq')
- grad_up: bfloat16 [8192, 24576], P('tensor', 'seq')
- grad_down: bfloat16 [24576, 8192], P('seq', 'tensor')
- grad_gain: float32 [8192], P('tensor')
- grad_router: float32 [8192], P('tensor')
Inputs may be any that keep to these rules, and one draw needn't show every extreme that they name: `slot_tokens`: slot p belongs to index p // 16 of seq; the live slots of one index hold distinct positions, the others hold arbitrary positions of that index. `live_counts`: in every draw some index of seq has all 16 slots live.
All inputs are finite; a program needn't handle non-finite values.
Results may differ from a plain program's by a relative error of at most 0.0077.
Values may be sent and summed in bfloat16 or wider, within the bound.
A program may use at most 128 MiB of HBM per device.

v0:
```python
import jax
import jax.numpy as jnp
from jax import lax
from jax.sharding import PartitionSpec as P

norm_eps = 1e-06


def silu_parts(gate):
    sig = jax.nn.sigmoid(gate)
    return (gate * sig, sig * (1.0 + gate * (1.0 - sig)))


def gate_backward(gate, upper, back, logits):
    act, slope = silu_parts(gate)
    hidden = act * upper
    weighted = (hidden * logits[:, None]).astype(jnp.bfloat16)
    router_grad = jnp.sum(hidden * back, axis=1)
    d_hidden = logits[:, None] * back
    d_gate = (d_hidden * upper * slope).astype(jnp.bfloat16)
    d_up = (d_hidden * act).astype(jnp.bfloat16)
    return (weighted, d_gate, d_up, router_grad)


def body(
    hidden_in,
    grad_out,
    slot_tokens,
    live_counts,
    norm_gain,
    router_weight,
    gate_weight,
    up_weight,
    down_weight,
):
    slot_count = slot_tokens.shape[0]
    width_total = hidden_in.shape[1] * lax.axis_size("tensor")
    live_rows = lax.iota(jnp.int32, slot_count) < live_counts[0]
    picked = jnp.take(hidden_in, slot_tokens, axis=0)
    upstream = jnp.where(
        live_rows[:, None], jnp.take(grad_out, slot_tokens, axis=0), jnp.zeros((), jnp.bfloat16)
    )
    wide = picked.astype(jnp.float32)
    squares = lax.psum(jnp.sum(wide * wide, axis=1), "tensor")
    inverse = lax.rsqrt(squares / width_total + norm_eps)[:, None]
    scaled = wide * inverse
    normed = (scaled * norm_gain).astype(jnp.bfloat16)
    all_normed, all_upstream = (
        lax.all_gather(normed, "seq", axis=0, tiled=True),
        lax.all_gather(upstream, "seq", axis=0, tiled=True),
    )
    gate_part = jnp.dot(all_normed, gate_weight, preferred_element_type=jnp.float32)
    upper_part = jnp.dot(all_normed, up_weight, preferred_element_type=jnp.float32)
    back_part = jnp.einsum(
        "pd,fd->pf", all_upstream, down_weight, preferred_element_type=jnp.float32
    )
    logit_part = jnp.dot(
        all_normed, router_weight.astype(jnp.bfloat16), preferred_element_type=jnp.float32
    )
    gate, upper, back, logits = (
        lax.psum_scatter(gate_part, "tensor", scatter_dimension=0, tiled=True),
        lax.psum_scatter(upper_part, "tensor", scatter_dimension=0, tiled=True),
        lax.psum_scatter(back_part, "tensor", scatter_dimension=0, tiled=True),
        lax.psum_scatter(logit_part, "tensor", scatter_dimension=0, tiled=True),
    )
    weighted, d_gate, d_up, router_grad = gate_backward(gate, upper, back, logits)
    weighted, d_gate, d_up = (
        lax.all_gather(weighted, "tensor", axis=0, tiled=True),
        lax.all_gather(d_gate, "tensor", axis=0, tiled=True),
        lax.all_gather(d_up, "tensor", axis=0, tiled=True),
    )
    router_grad = lax.all_gather(router_grad, "tensor", axis=0, tiled=True)
    grad_gate = jnp.einsum("pd,pf->df", all_normed, d_gate, preferred_element_type=jnp.float32)
    grad_up = jnp.einsum("pd,pf->df", all_normed, d_up, preferred_element_type=jnp.float32)
    grad_down = jnp.einsum("pf,pd->fd", weighted, all_upstream, preferred_element_type=jnp.float32)
    router_part = jnp.dot(
        router_grad, all_normed.astype(jnp.float32), precision=lax.Precision.HIGHEST
    )
    total = jnp.einsum("pf,df->pd", d_gate, gate_weight, preferred_element_type=jnp.float32)
    total = total + jnp.einsum("pf,df->pd", d_up, up_weight, preferred_element_type=jnp.float32)
    d_normed = lax.psum_scatter(
        total + router_grad[:, None] * router_weight, "seq", scatter_dimension=0, tiled=True
    )
    d_scaled = d_normed * norm_gain
    inner = lax.psum(jnp.sum(d_scaled * scaled, axis=1), "tensor") / width_total
    d_picked = inverse * (d_scaled - scaled * inner[:, None])
    d_picked = jnp.where(live_rows[:, None], d_picked, jnp.zeros((), jnp.float32))
    gain_part = jnp.sum(d_normed * scaled, axis=0)
    gain_total, router_total, count_total = lax.psum(
        (gain_part, router_part, live_counts[0].astype(jnp.float32)), "seq"
    )
    count_scale = lax.rsqrt(count_total)
    grad_in = grad_out.astype(jnp.float32).at[slot_tokens].add(d_picked).astype(jnp.bfloat16)
    gate_out = (count_scale * grad_gate).astype(jnp.bfloat16)
    up_out = (count_scale * grad_up).astype(jnp.bfloat16)
    down_out = (count_scale * grad_down).astype(jnp.bfloat16)
    return (
        grad_in,
        gate_out,
        up_out,
        down_out,
        count_scale * gain_total,
        count_scale * router_total,
    )


def solution(mesh):
    in_specs = (
        P("seq", "tensor"),
        P("seq", "tensor"),
        P("seq"),
        P("seq"),
        P("tensor"),
        P("tensor"),
        P("tensor", "seq"),
        P("tensor", "seq"),
        P("seq", "tensor"),
    )
    out_specs = (
        P("seq", "tensor"),
        P("tensor", "seq"),
        P("tensor", "seq"),
        P("seq", "tensor"),
        P("tensor"),
        P("tensor"),
    )
    return jax.shard_map(body, mesh=mesh, in_specs=in_specs, out_specs=out_specs, check_vma=False)
```

profile of v0, /device:TPU:0, one launch (start us, length us, event | category | flops | bytes accessed | tf_op | source)
XLA Modules:
  0.0 345.2 jit_solution(15996386094158586159)
XLA Ops:
  9.3 1.8 gather_fusion.1
  11.1 33.0 %all_gather.19 = bf16[128,2048]{1,0:T(8,128)(2,1)S(1)} all-gather(bf16[16,2048]{1,0:T(8,128)(2,1)S(1)} %select_select_fusion), channel_id=1, replica_groups=mesh['seq'=8,'tensor'=4] {'seq'}, dimensions={0}, use_global_device_ids=true | all-gather | bytes 589824 | tf_op jit(solution)/shard_map/all_gather | solution.py:50
  44.2 10.0 %fusion.24 = f32[128,3072]{1,0:T(8,128)} fusion(bf16[128,2048]{1,0:T(8,128)(2,1)S(1)} %all_gather.19, bf16[3072,2048]{1,0:T(8,128)(2,1)} %param.19), kind=kOutput, calls=%fused_computation.48 | convolution fusion | flops 1610612736 | bytes 14680064 | tf_op jit(solution)/shard_map/pd,fd->pf/dot_general | solution.py:54
  55.0 5.7 %psum.35 = f32[16]{0:T(128)S(1)} all-reduce(f32[16]{0:T(128)S(1)} %fusion.14), channel_id=1, replica_groups=mesh['seq'=8,'tensor'=4] {'tensor'}, use_global_device_ids=true, to_apply=%region_1.3 | all-reduce | flops 16 | bytes 128 | tf_op jit(solution)/shard_map/psum | solution.py:44
  60.8 31.3 %all_gather.18 = bf16[128,2048]{1,0:T(8,128)(2,1)S(1)} all-gather(bf16[16,2048]{1,0:T(8,128)(2,1)S(1)} %fusion.6), channel_id=1, replica_groups=mesh['seq'=8,'tensor'=4] {'seq'}, dimensions={0}, use_global_device_ids=true | all-gather | bytes 589824 | tf_op jit(solution)/shard_map/all_gather | solution.py:49
  92.1 7.5 %fusion.26 = f32[128,3072]{1,0:T(8,128)} fusion(bf16[128,2048]{1,0:T(8,128)(2,1)S(1)} %all_gather.18, bf16[2048,3072]{1,0:T(8,128)(2,1)} %param.17), kind=kOutput, calls=%fused_computation.50 | convolution fusion | flops 1610612736 | bytes 14680064 | tf_op jit(solution)/shard_map/dot_general | solution.py:52
  99.7 7.5 %fusion.25 = f32[128,3072]{1,0:T(8,128)} fusion(bf16[128,2048]{1,0:T(8,128)(2,1)S(1)} %all_gather.18, bf16[2048,3072]{1,0:T(8,128)(2,1)} %param.18), kind=kOutput, calls=%fused_computation.49 | convolution fusion | flops 1610612736 | bytes 14680064 | tf_op jit(solution)/shard_map/dot_general | solution.py:53
  109.5 19.7 %reduce-scatter.9.cloned.1.call-done = f32[32,3072]{1,0:T(8,128)} async-done(((f32[128,3072]{1,0:T(8,128)}), f32[32,3072]{1,0:T(8,128)}) %reduce-scatter.9.cloned.1.call-update) | async-done | bytes 393232 | tf_op jit(solution)/shard_map/reduce_scatter | solution.py:61
  129.2 31.2 %reduce-scatter.7.cloned.1.call-done = f32[32,3072]{1,0:T(8,128)} async-done(((f32[128,3072]{1,0:T(8,128)}), f32[32,3072]{1,0:T(8,128)}) %reduce-scatter.7.cloned.1.call-update) | async-done | bytes 393232 | tf_op jit(solution)/shard_map/reduce_scatter | solution.py:62
  162.0 5.7 %all-reduce.3 = (f32[128]{0:T(128)S(1)}, f32[128]{0:T(128)S(1)}) all-reduce(f32[128]{0:T(128)S(1)} %convolution_bitcast_fusion, f32[128]{0:T(128)S(1)} %dynamic-update-slice), channel_id=2, replica_groups=mesh['seq'=8,'tensor'=4] {'tensor'}, use_global_device_ids=true, to_apply=%region_2.4.clone | all-reduce | flops 256 | bytes 2048
  167.9 1.5 multiply_convert_fusion.3
  169.3 8.3 %all_gather.20 = bf16[128,3072]{1,0:T(8,128)(2,1)S(1)} all-gather(bf16[32,3072]{1,0:T(8,128)(2,1)S(1)} %get-tuple-element.15), channel_id=1, replica_groups=mesh['seq'=8,'tensor'=4] {'tensor'}, dimensions={0}, use_global_device_ids=true | all-gather | bytes 983040 | tf_op jit(solution)/shard_map/all_gather | solution.py:69
  177.6 8.9 %all_gather.21 = bf16[128,3072]{1,0:T(8,128)(2,1)S(1)} all-gather(bf16[32,3072]{1,0:T(8,128)(2,1)S(1)} %get-tuple-element.16), channel_id=1, replica_groups=mesh['seq'=8,'tensor'=4] {'tensor'}, dimensions={0}, use_global_device_ids=true | all-gather | bytes 983040 | tf_op jit(solution)/shard_map/all_gather | solution.py:70
  186.5 8.9 %fusion.27 = f32[128,2048]{1,0:T(8,128)S(1)} fusion(bf16[128,3072]{1,0:T(8,128)(2,1)S(1)} %all_gather.20, bf16[2048,3072]{1,0:T(8,128)(2,1)} %param.17), kind=kOutput, calls=%fused_computation.51 | convolution fusion | flops 1610612736 | bytes 14417920 | tf_op jit(solution)/shard_map/pf,df->pd/dot_general | solution.py:79
  195.4 9.8 %fusion = f32[128,2048]{1,0:T(8,128)} fusion(f32[128,2048]{1,0:T(8,128)S(1)} %fusion.27, bf16[128,3072]{1,0:T(8,128)(2,1)S(1)} %all_gather.21, bf16[2048,3072]{1,0:T(8,128)(2,1)} %param.18, f32[2048]{0:T(1024)S(1)} %copy-done.6, f32[128]{0:T(128)S(1)} %get-tuple-element.13), kind=kOutput, calls=%fused_computation.7 | convolution fusion | flops 1611399168 | bytes 15475200 | tf_op jit(solution)/shard_map/pf,df->pd/dot_general | solution.py:80
  206.6 9.1 %all_gather.23 = bf16[128,3072]{1,0:T(8,128)(2,1)} all-gather(bf16[32,3072]{1,0:T(8,128)(2,1)S(1)} %get-tuple-element.14), channel_id=1, replica_groups=mesh['seq'=8,'tensor'=4] {'tensor'}, dimensions={0}, use_global_device_ids=true | all-gather | bytes 983040 | tf_op jit(solution)/shard_map/all_gather | solution.py:68
  215.8 54.3 %reduce-scatter.11.cloned.1.call-done = f32[16,2048]{1,0:T(8,128)} async-done(((f32[128,2048]{1,0:T(8,128)}), f32[16,2048]{1,0:T(8,128)}) %reduce-scatter.11.cloned.1.call-update) | async-done | bytes 131088 | tf_op jit(solution)/shard_map/reduce_scatter | solution.py:81
  271.2 35.6 %all-reduce.2 = (f32[]{:T(128)}, f32[2048]{0:T(1024)S(1)}, f32[2048]{0:T(1024)S(1)}) all-reduce(f32[]{:T(128)S(6)} %convert_element_type.44, f32[2048]{0:T(1024)S(1)} %get-tuple-element.7, f32[2048]{0:T(1024)S(1)} %bitcast.30), channel_id=1, replica_groups=mesh['seq'=8,'tensor'=4] {'seq'}, use_global_device_ids=true, to_apply=%region_11.13 | all-reduce | flops 4097 | bytes 32776 | tf_op jit(solution)/shard_map/psum | solution.py:89
  307.5 6.6 %multiply_convert_fusion.1 = bf16[2048,3072]{1,0:T(8,128)(2,1)} fusion(f32[]{:T(128)S(6)} %rsqrt.7, bf16[128,2048]{1,0:T(8,128)(2,1)S(1)} %all_gather.18, bf16[128,3072]{1,0:T(8,128)(2,1)S(1)} %all_gather.21), kind=kOutput, calls=%fused_computation.4 | convolution fusion | flops 1623195648 | bytes 13893636 | tf_op jit(solution)/shard_map/pd,pf->df/dot_general | solution.py:74
  314.1 6.6 %multiply_convert_fusion.2 = bf16[2048,3072]{1,0:T(8,128)(2,1)} fusion(f32[]{:T(128)S(6)} %rsqrt.7, bf16[128,2048]{1,0:T(8,128)(2,1)S(1)} %all_gather.18, bf16[128,3072]{1,0:T(8,128)(2,1)S(1)} %all_gather.20), kind=kOutput, calls=%fused_computation.5 | convolution fusion | flops 1623195648 | bytes 13893636 | tf_op jit(solution)/shard_map/pd,pf->df/dot_general | solution.py:73
  320.7 5.6 %psum.36 = f32[16]{0:T(128)S(1)} all-reduce(f32[16]{0:T(128)S(1)} %get-tuple-element.8), channel_id=1, replica_groups=mesh['seq'=8,'tensor'=4] {'tensor'}, use_global_device_ids=true, to_apply=%region_9.11 | all-reduce | flops 16 | bytes 128 | tf_op jit(solution)/shard_map/psum | solution.py:85
  326.4 3.0 scatter_custom_fusion
  329.4 2.1 convert_element_type.43
  331.5 6.6 %multiply_convert_fusion = bf16[3072,2048]{1,0:T(8,128)(2,1)} fusion(f32[]{:T(128)S(6)} %rsqrt.7, bf16[128,3072]{1,0:T(8,128)(2,1)S(1)} %copy-done.2, bf16[128,2048]{1,0:T(8,128)(2,1)S(1)} %all_gather.19), kind=kOutput, calls=%fused_computation.3 | convolution fusion | flops 1623195648 | bytes 13893636 | tf_op jit(solution)/shard_map/pf,pd->fd/dot_general | solution.py:75
  (47 shorter events, 8.4 us)
Async XLA Ops:
  7.2 47.0 %copy-start = (bf16[128,2048]{1,0:T(8,128)(2,1)S(1)}, bf16[128,2048]{1,0:T(8,128)(2,1)}, u32[]{:S(2)}) copy-start(bf16[128,2048]{1,0:T(8,128)(2,1)} %param.11) | copy-start | bytes 1572868
  7.2 53.5 %copy-start.5 = (f32[2048]{0:T(1024)S(1)}, f32[2048]{0:T(1024)}, u32[]{:S(2)}) copy-start(f32[2048]{0:T(1024)} %param.15) | copy-start | bytes 24580
  7.2 102.3 %reduce-scatter.5.cloned.1.call-start = ((), (), s32[]{:S(2)}) async-start(), calls=%async_computation.4 | async-start | bytes 1966080 | tf_op jit(solution)/shard_map/reduce_scatter | solution.py:63
  54.2 75.0 %reduce-scatter.9.cloned.1.call-start = ((), (), s32[]{:S(2)}) async-start(), calls=%async_computation.6 | async-start | bytes 1966080 | tf_op jit(solution)/shard_map/reduce_scatter | solution.py:61
  99.6 7.7 %copy-start.7 = (u32[32]{0:T(128)S(1)}, u32[32]{0:T(128)}, u32[]{:S(2)}) copy-start(u32[32]{0:T(128)} %constant.29) | copy-start | bytes 388
  99.6 8.9 %copy-start.6 = (f32[2048]{0:T(1024)S(1)}, f32[2048]{0:T(1024)}, u32[]{:S(2)}) copy-start(f32[2048]{0:T(1024)} %param.16) | copy-start | bytes 24580
  99.7 60.7 %reduce-scatter.7.cloned.1.call-start = ((), (), s32[]{:S(2)}) async-start(), calls=%async_computation.5 | async-start | bytes 1966080 | tf_op jit(solution)/shard_map/reduce_scatter | solution.py:62
  107.3 162.8 %reduce-scatter.11.cloned.1.call-start = ((), (), s32[]{:S(2)}) async-start(), calls=%async_computation.7 | async-start | bytes 1179648 | tf_op jit(solution)/shard_map/reduce_scatter | solution.py:81
  186.5 18.7 %copy-start.3 = (bf16[128,2048]{1,0:T(8,128)(2,1)S(1)}, bf16[128,2048]{1,0:T(8,128)(2,1)}, u32[]{:S(2)}) copy-start(bf16[128,2048]{1,0:T(8,128)(2,1)} %param.12) | copy-start | bytes 1572868
  314.1 12.3 %copy-start.4 = (f32[16,2048]{1,0:T(8,128)S(1)}, f32[16,2048]{1,0:T(8,128)}, u32[]{:S(2)}) copy-start(f32[16,2048]{1,0:T(8,128)} %reduce-scatter.11.cloned.1.call-done) | copy-start | bytes 393220
  314.1 17.4 %copy-start.2 = (bf16[128,3072]{1,0:T(8,128)(2,1)S(1)}, bf16[128,3072]{1,0:T(8,128)(2,1)}, u32[]{:S(2)}) copy-start(bf16[128,3072]{1,0:T(8,128)(2,1)} %all_gather.23) | copy-start | bytes 2359300
  314.1 24.6 %copy-start.1 = (bf16[128,2048]{1,0:T(8,128)(2,1)S(1)}, bf16[128,2048]{1,0:T(8,128)(2,1)}, u32[]{:S(2)}) copy-start(bf16[128,2048]{1,0:T(8,128)(2,1)} %param.11) | copy-start | bytes 1572868
Sparse Core Ops, SparseCore 0:
  54.3 29.1 reduce-scatter.4
  99.8 29.3 reduce-scatter.8
  132.3 28.0 reduce-scatter.6
  205.3 64.6 reduce-scatter.10
where the time goes:
time: 346 us; the launch traced here: 345 us
  blocking collectives  143 us (41%)
  waiting for transfers between devices  105 us (30%)
  matrix products  64 us (18%)
  between operations  16.6 us (5%)
  other arithmetic  12.6 us (4%)
    reduce_scatter x1, waiting for transfers between devices, body(): lax.psum_scatter(total + router_grad[:, None] * router_weight, 'seq', sca...  54.3 us
    psum x1, blocking collectives, body(): lax.psum((gain_part, router_part, live_counts[0].astype(jnp.float32)), 's...  35.6 us
    all_gather x1, blocking collectives, body(): lax.all_gather(upstream, 'seq', axis=0, tiled=True)  33 us
    all_gather x1, blocking collectives, body(): lax.all_gather(normed, 'seq', axis=0, tiled=True)  31.3 us
    reduce_scatter x1, waiting for transfers between devices, body(): lax.psum_scatter(upper_part, 'tensor', scatter_dimension=0, tiled=True)  31.2 us
    reduce_scatter x1, waiting for transfers between devices, body(): lax.psum_scatter(gate_part, 'tensor', scatter_dimension=0, tiled=True)  19.7 us
    dot_general x1, matrix products, body(): jnp.einsum('pd,fd->pf', all_upstream, down_weight, preferred_element_type...  9.95 us
    dot_general x1, matrix products, body(): jnp.einsum('pf,df->pd', d_up, up_weight, preferred_element_type=jnp.float32)  9.79 us
  transfers between devices with their start and end apart: 4, of which 3 were waited for; matrix products, arithmetic and copies ran while one was open for 5% of the time, Pallas kernels for 0%

commit v1 on v0

v1 whole, which is shorter than its diff:
```python
import functools

import jax
import jax.numpy as jnp
from jax import lax
from jax.experimental import pallas as pl
from jax.experimental.pallas import tpu as pltpu
from jax.sharding import PartitionSpec as P

norm_eps = 1e-06
f32 = jnp.float32
bf16 = jnp.bfloat16
MESH = pl.DeviceIdType.MESH


def pick_chunks(size, options, unit=128):
    for n in options:
        if size % (n * unit) == 0:
            return n
    return 1


def nt_dot(a, b):
    return lax.dot_general(a, b, (((1,), (1,)), ((), ())), preferred_element_type=f32)


def kernel(
    ns,
    nt,
    nc,
    nk,
    hid,
    gout,
    tok_col,
    tok_row,
    live,
    gain,
    router,
    wg_hbm,
    wu_hbm,
    wd_hbm,
    o_in,
    o_gr,
    o_w,
    o_dg,
    o_du,
    o_norm,
    o_ups,
    o_cs,
    wg,
    wu,
    wd,
    gath,
    colbuf,
    invbuf,
    logbuf,
    rgbuf,
    rgacc,
    smsg,
    srec,
    imsg,
    irec,
    part,
    drec,
    xsnd,
    xrec,
    acc,
    ysnd,
    yrec,
    zsnd,
    zrec,
    gmsg,
    grec,
    w_sem,
    agz_s,
    agz_r,
    agy_s,
    agy_r,
    sm_s,
    sm_r,
    in_s,
    in_r,
    d_s,
    d_r,
    x_s,
    x_r,
    a_s,
    a_r,
    rg_s,
    rg_r,
    y_s,
    y_r,
    z_s,
    z_r,
    g_s,
    g_r,
):
    tokens, width = hid.shape
    cap = tok_col.shape[0]
    rows = ns * cap
    half = rows // 2
    hidden = wg.shape[1]
    fc = hidden // nc
    kc = width // nk
    nz, nx = ns // 2, nt // 2
    s, t = lax.axis_index("seq"), lax.axis_index("tensor")
    y, z = lax.rem(s, 2), lax.div(s, 2)
    core, x = lax.rem(t, 2), lax.div(t, 2)
    mate = t + 1 - 2 * core
    yp = s + 1 - 2 * y
    mine = pl.multiple_of(core * half, half)

    def remote(src, dst, ssem, rsem, **where):
        return pltpu.make_async_remote_copy(
            src_ref=src,
            dst_ref=dst,
            send_sem=ssem,
            recv_sem=rsem,
            device_id=where,
            device_id_type=MESH,
        )

    loads = [
        pltpu.make_async_copy(wd_hbm, wd, w_sem.at[0]),
        pltpu.make_async_copy(wg_hbm, wg, w_sem.at[1]),
        pltpu.make_async_copy(wu_hbm, wu, w_sem.at[2]),
    ]
    for load in loads:
        load.start()

    barrier = pltpu.get_barrier_semaphore()
    for j in range(1, ns):
        pl.semaphore_signal(
            barrier, inc=1, device_id={"seq": lax.rem(s + j, ns)}, device_id_type=MESH
        )
    for j in range(1, nt):
        pl.semaphore_signal(
            barrier, inc=1, device_id={"tensor": lax.rem(t + j, nt)}, device_id_type=MESH
        )

    hot = (tok_col[...] == lax.broadcasted_iota(jnp.int32, (cap, tokens), 1)).astype(f32)
    live_col = (lax.broadcasted_iota(jnp.int32, (cap, 1), 0) < live[...]).astype(f32)
    gath[s, :, pl.ds(0, width)] = jnp.dot(
        hot.astype(bf16), hid[...], preferred_element_type=f32
    ).astype(bf16)
    gath[s, :, pl.ds(width, width)] = jnp.dot(
        (hot * live_col).astype(bf16), gout[...], preferred_element_type=f32
    ).astype(bf16)
    gath[s, :, pl.ds(2 * width, 128)] = jnp.broadcast_to(
        live[...].astype(f32), (cap, 128)
    ).astype(bf16)
    pl.semaphore_wait(barrier, ns - 1 + nt - 1)

    def agz(j):
        own = gath.at[s]
        return remote(own, own, agz_s.at[j], agz_r.at[j], seq=2 * lax.rem(z + j, nz) + y)

    def agy(j):
        block = gath.at[2 * lax.rem(z + nz - j, nz) + y]
        return remote(block, block, agy_s.at[j], agy_r.at[j], seq=yp)

    def consume(b):
        rows_b = pl.ds(pl.multiple_of(b * cap, cap), cap)
        wide = gath[b, :, pl.ds(0, width)].astype(f32)
        o_ups[rows_b, :] = gath[b, :, pl.ds(width, width)]
        colbuf[rows_b, :] = jnp.broadcast_to(
            jnp.sum(wide * wide, axis=1, keepdims=True), (cap, 128)
        )

    agy(0).start()
    for j in range(1, nz):
        agz(j).start()
    consume(s)

    @pl.loop(1, nz)
    def _(j):
        agz(j).wait_recv()
        agy(j).start()
        consume(2 * lax.rem(z + nz - j, nz) + y)

    @pl.loop(0, nz)
    def _(j):
        agy(j).wait_recv()
        consume(2 * lax.rem(z + nz - j, nz) + 1 - y)

    def small(k, j):
        return remote(
            smsg.at[k], srec.at[k, j], sm_s.at[k, j], sm_r.at[k, j], tensor=lax.rem(t + j, nt)
        )

    def small_send(k):
        smsg[k] = colbuf[...].T[0:8, :]
        for j in range(1, nt):
            small(k, j).start()

    def small_sum(k):
        total = smsg[k]
        for j in range(1, nt):
            small(k, j).wait_recv()
            total = total + srec[k, j]
        return jnp.broadcast_to(total[0:1, :], (128, rows)).T

    small_send(0)

    def pair(a, c):
        return remote(
            part.at[a, c, 1 - core], drec.at[a, c], d_s.at[a, c], d_r.at[a, c], tensor=mate
        )

    def cross(j, a, c):
        return remote(
            xsnd.at[a, c],
            xrec.at[j, a, c],
            x_s.at[j, a, c],
            x_r.at[j, a, c],
            tensor=2 * lax.rem(x + j, nx) + core,
        )

    def emit(a, c, value):
        part[a, c] = value.reshape(2, half, fc)
        pair(a, c).start()

    def relay(a, c):
        pair(a, c).wait_recv()
        total = part[a, c, core] + drec[a, c]
        part[a, c, core] = total
        xsnd[a, c] = total.astype(bf16)
        for j in range(1, nx):
            cross(j, a, c).start()

    def cols(c):
        return pl.ds(pl.multiple_of(c * fc, fc), fc)

    loads[0].wait()

    @pl.loop(0, nc)
    def _(c):
        emit(0, c, nt_dot(o_ups[...], wd[cols(c), :]))

        @pl.when(c > 0)
        def _():
            relay(0, c - 1)

    relay(0, nc - 1)

    width_total = width * nt
    invbuf[...] = lax.rsqrt(small_sum(0) / width_total + norm_eps)
    router_row = router[...].astype(bf16).astype(f32)

    @pl.loop(0, ns)
    def _(b):
        rows_b = pl.ds(pl.multiple_of(b * cap, cap), cap)
        scaled = gath[b, :, pl.ds(0, width)].astype(f32) * invbuf[rows_b, 0:1]
        normed = (scaled * gain[...]).astype(bf16)
        o_norm[rows_b, :] = normed
        colbuf[rows_b, :] = jnp.broadcast_to(
            jnp.sum(normed.astype(f32) * router_row, axis=1, keepdims=True), (cap, 128)
        )

    small_send(1)
    loads[1].wait()
    loads[2].wait()

    @pl.loop(0, nc)
    def _(c):
        emit(1, c, jnp.dot(o_norm[...], wg[:, cols(c)], preferred_element_type=f32))

        @pl.when(c > 0)
        def _():
            relay(2, c - 1)

        emit(2, c, jnp.dot(o_norm[...], wu[:, cols(c)], preferred_element_type=f32))
        relay(1, c)

    relay(2, nc - 1)

    logbuf[...] = small_sum(1)
    rgacc[...] = jnp.zeros_like(rgacc)
    acc[...] = jnp.zeros_like(acc)
    acts = (o_w, o_dg, o_du)

    def act_copy(a, c):
        piece = acts[a].at[pl.ds(mine, half), cols(c)]
        return remote(piece, piece, a_s.at[a, c], a_r.at[a, c], tensor=mate)

    def gate_backward(c):
        for a in range(3):
            for j in range(1, nx):
                cross(j, a, c).wait_recv()

        @pl.loop(0, half // 16)
        def _(r):
            sub = pl.ds(pl.multiple_of(r * 16, 16), 16)
            out = pl.ds(pl.multiple_of(mine + r * 16, 16), 16)
            back, gate, upper = [
                functools.reduce(
                    lambda u, v: u + v,
                    [xrec[j, a, c, sub, :].astype(f32) for j in range(1, nx)],
                    part[a, c, core, sub, :],
                )
                for a in range(3)
            ]
            logit = logbuf[out, 0:1]
            sig = jax.nn.sigmoid(gate)
            act = gate * sig
            slope = sig * (1.0 + gate * (1.0 - sig))
            hid_v = act * upper
            o_w[out, cols(c)] = (hid_v * logit).astype(bf16)
            d_hidden = logit * back
            o_dg[out, cols(c)] = (d_hidden * upper * slope).astype(bf16)
            o_du[out, cols(c)] = (d_hidden * act).astype(bf16)
            terms = hid_v * back
            add = terms[:, 0:128]
            for i in range(1, fc // 128):
                add = add + terms[:, i * 128 : (i + 1) * 128]
            rgacc[sub, :] = rgacc[sub, :] + add

        for a in range(3):
            act_copy(a, c).start()

    def kcols(k):
        return pl.ds(pl.multiple_of(k * kc, kc), kc)

    def back_dots(c, k):
        return nt_dot(o_dg[:, cols(c)], wg[kcols(k), cols(c)]) + nt_dot(
            o_du[:, cols(c)], wu[kcols(k), cols(c)]
        )

    def act_wait(c):
        for a in range(3):
            act_copy(a, c).wait_recv()

    @pl.loop(0, nc)
    def _(c):
        gate_backward(c)

        @pl.when(c > 0)
        def _():
            act_wait(c - 1)

            @pl.loop(0, nk)
            def _(k):
                acc[:, :, kcols(k)] = acc[:, :, kcols(k)] + back_dots(c - 1, k).reshape(
                    ns, cap, kc
                )

    rgbuf[core] = jnp.broadcast_to(jnp.sum(rgacc[...], axis=1, keepdims=True), (half, 128))
    rg_copy = remote(rgbuf.at[core], rgbuf.at[core], rg_s, rg_r, tensor=mate)
    rg_copy.start()
    act_wait(nc - 1)
    rg_copy.wait_recv()

    def ycopy(k):
        return remote(ysnd.at[k], yrec.at[k], y_s.at[k], y_r.at[k], seq=yp)

    def zcopy(j, k):
        return remote(
            zsnd.at[j, k],
            zrec.at[j, k],
            z_s.at[j, k],
            z_r.at[j, k],
            seq=2 * lax.rem(z + j, nz) + y,
        )

    def zstage(k):
        ycopy(k).wait_recv()
        for j in range(1, nz):
            zz = lax.rem(z + j, nz)
            zsnd[j, k] = (acc[2 * zz + y, :, kcols(k)] + yrec[k, zz].astype(f32)).astype(bf16)
            zcopy(j, k).start()
        acc[s, :, kcols(k)] = acc[s, :, kcols(k)] + yrec[k, z].astype(f32)

    @pl.loop(0, nk)
    def _(k):
        rg = jnp.concatenate([rgbuf[0], rgbuf[1]], axis=0)[:, 0:1]
        total = back_dots(nc - 1, k) + rg * router[:, kcols(k)]
        acc[:, :, kcols(k)] = acc[:, :, kcols(k)] + total.reshape(ns, cap, kc)
        for zz in range(nz):
            ysnd[k, zz] = acc[2 * zz + 1 - y, :, kcols(k)].astype(bf16)
        ycopy(k).start()

        @pl.when(k > 0)
        def _():
            zstage(k - 1)

    zstage(nk - 1)

    router_part = jnp.zeros((1, width), f32)
    count = jnp.zeros((1, 128), f32)
    rg_all = jnp.concatenate([rgbuf[0], rgbuf[1]], axis=0)
    for b in range(ns):
        block = o_norm[b * cap : (b + 1) * cap, :].astype(f32)
        router_part = router_part + jnp.sum(
            rg_all[b * cap : (b + 1) * cap, 0:1] * block, axis=0, keepdims=True
        )
        count = count + gath[b, 0:1, 2 * width : 2 * width + 128].astype(f32)
    scale = lax.rsqrt(count)
    o_cs[...] = scale
    gmsg[1:2, :] = router_part

    for j in range(1, nz):

        @pl.loop(0, nk)
        def _(k):
            zcopy(j, k).wait_recv()
            acc[s, :, kcols(k)] = acc[s, :, kcols(k)] + zrec[j, k].astype(f32)

    own = pl.ds(pl.multiple_of(s * cap, cap), cap)
    inverse = invbuf[own, 0:1]
    scaled = gath[s, :, pl.ds(0, width)].astype(f32) * inverse
    d_normed = acc[s]
    d_scaled = d_normed * gain[...]
    imsg[...] = jnp.broadcast_to(jnp.sum(d_scaled * scaled, axis=1, keepdims=True), (cap, 128))

    def inner_copy(j):
        return remote(imsg, irec.at[j], in_s.at[j], in_r.at[j], tensor=lax.rem(t + j, nt))

    def gain_copy(j):
        return remote(gmsg, grec.at[j], g_s.at[j], g_r.at[j], seq=lax.rem(s + j, ns))

    for j in range(1, nt):
        inner_copy(j).start()
    gmsg[0:1, :] = jnp.sum(d_normed * scaled, axis=0, keepdims=True)
    for j in range(1, ns):
        gain_copy(j).start()

    inner = imsg[...]
    for j in range(1, nt):
        inner_copy(j).wait_recv()
        inner = inner + irec[j]
    inner = inner[:, 0:1] / width_total
    d_picked = inverse * (d_scaled - scaled * inner) * live_col
    place = (tok_row[...] == lax.broadcasted_iota(jnp.int32, (tokens, cap), 0)).astype(f32)
    added = jnp.dot(place, d_picked, precision=lax.Precision.HIGHEST, preferred_element_type=f32)
    o_in[...] = (gout[...].astype(f32) + added).astype(bf16)

    total = gmsg[...]
    for j in range(1, ns):
        gain_copy(j).wait_recv()
        total = total + grec[j]
    o_gr[...] = total * scale[:, 0:1]

    agy(0).wait_send()
    for j in range(1, nz):
        agz(j).wait_send()
        agy(j).wait_send()
    for j in range(1, nt):
        small(0, j).wait_send()
        small(1, j).wait_send()
        inner_copy(j).wait_send()
    for j in range(1, ns):
        gain_copy(j).wait_send()
    rg_copy.wait_send()

    @pl.loop(0, nc)
    def _(c):
        for a in range(3):
            pair(a, c).wait_send()
            act_copy(a, c).wait_send()
            for j in range(1, nx):
                cross(j, a, c).wait_send()

    @pl.loop(0, nk)
    def _(k):
        ycopy(k).wait_send()
        for j in range(1, nz):
            zcopy(j, k).wait_send()


def body(
    hidden_in,
    grad_out,
    slot_tokens,
    live_counts,
    norm_gain,
    router_weight,
    gate_weight,
    up_weight,
    down_weight,
):
    ns, nt = lax.axis_size("seq"), lax.axis_size("tensor")
    cap = slot_tokens.shape[0]
    tokens, width = hidden_in.shape
    hidden = gate_weight.shape[1]
    rows, nz, nx = ns * cap, ns // 2, nt // 2
    half = rows // 2
    nc = pick_chunks(hidden, (6, 4, 3, 2))
    nk = pick_chunks(width, (4, 2))
    fc, kc = hidden // nc, width // nk
    vmem = pl.BlockSpec(memory_space=pltpu.VMEM)
    hbm = pl.BlockSpec(memory_space=pl.ANY)
    dma = pltpu.SemaphoreType.DMA
    grad_in, small, weighted, d_gate, d_up, normed, upstream, scale = pl.pallas_call(
        functools.partial(kernel, ns, nt, nc, nk),
        out_shape=[
            jax.ShapeDtypeStruct((tokens, width), bf16),
            jax.ShapeDtypeStruct((2, width), f32),
            jax.ShapeDtypeStruct((rows, hidden), bf16),
            jax.ShapeDtypeStruct((rows, hidden), bf16),
            jax.ShapeDtypeStruct((rows, hidden), bf16),
            jax.ShapeDtypeStruct((rows, width), bf16),
            jax.ShapeDtypeStruct((rows, width), bf16),
            jax.ShapeDtypeStruct((1, 128), f32),
        ],
        in_specs=[vmem] * 7 + [hbm] * 3,
        out_specs=[vmem] * 8,
        scratch_shapes=[
            pltpu.VMEM((width, hidden), bf16),
            pltpu.VMEM((width, hidden), bf16),
            pltpu.VMEM((hidden, width), bf16),
            pltpu.VMEM((ns, cap, 2 * width + 128), bf16),
            pltpu.VMEM((rows, 128), f32),
            pltpu.VMEM((rows, 128), f32),
            pltpu.VMEM((rows, 128), f32),
            pltpu.VMEM((2, half, 128), f32),
            pltpu.VMEM((half, 128), f32),
            pltpu.VMEM((2, 8, rows), f32),
            pltpu.VMEM((2, nt, 8, rows), f32),
            pltpu.VMEM((cap, 128), f32),
            pltpu.VMEM((nt, cap, 128), f32),
            pltpu.VMEM((3, nc, 2, half, fc), f32),
            pltpu.VMEM((3, nc, half, fc), f32),
            pltpu.VMEM((3, nc, half, fc), bf16),
            pltpu.VMEM((nx, 3, nc, half, fc), bf16),
            pltpu.VMEM((ns, cap, width), f32),
            pltpu.VMEM((nk, nz, cap, kc), bf16),
            pltpu.VMEM((nk, nz, cap, kc), bf16),
            pltpu.VMEM((nz, nk, cap, kc), bf16),
            pltpu.VMEM((nz, nk, cap, kc), bf16),
            pltpu.VMEM((2, width), f32),
            pltpu.VMEM((ns, 2, width), f32),
            dma((3,)),
            dma((nz,)),
            dma((nz,)),
            dma((nz,)),
            dma((nz,)),
            dma((2, nt)),
            dma((2, nt)),
            dma((nt,)),
            dma((nt,)),
            dma((3, nc)),
            dma((3, nc)),
            dma((nx, 3, nc)),
            dma((nx, 3, nc)),
            dma((3, nc)),
            dma((3, nc)),
            dma,
            dma,
            dma((nk,)),
            dma((nk,)),
            dma((nz, nk)),
            dma((nz, nk)),
            dma((ns,)),
            dma((ns,)),
        ],
        compiler_params=pltpu.CompilerParams(
            collective_id=0, has_side_effects=True, vmem_limit_bytes=67_043_328
        ),
    )(
        hidden_in,
        grad_out,
        slot_tokens.reshape(cap, 1),
        slot_tokens.reshape(1, cap),
        live_counts.reshape(1, 1),
        norm_gain.reshape(1, width),
        router_weight.reshape(1, width),
        gate_weight,
        up_weight,
        down_weight,
    )
    count_scale = scale[0, 0]
    grad_gate = jnp.einsum("pd,pf->df", normed, d_gate, preferred_element_type=f32)
    grad_up = jnp.einsum("pd,pf->df", normed, d_up, preferred_element_type=f32)
    grad_down = jnp.einsum("pf,pd->fd", weighted, upstream, preferred_element_type=f32)
    return (
        grad_in,
        (count_scale * grad_gate).astype(bf16),
        (count_scale * grad_up).astype(bf16),
        (count_scale * grad_down).astype(bf16),
        small[0],
        small[1],
    )


def solution(mesh):
    in_specs = (
        P("seq", "tensor"),
        P("seq", "tensor"),
        P("seq"),
        P("seq"),
        P("tensor"),
        P("tensor"),
        P("tensor", "seq"),
        P("tensor", "seq"),
        P("seq", "tensor"),
    )
    out_specs = (
        P("seq", "tensor"),
        P("tensor", "seq"),
        P("tensor", "seq"),
        P("seq", "tensor"),
        P("tensor"),
        P("tensor"),
    )
    return jax.shard_map(body, mesh=mesh, in_specs=in_specs, out_specs=out_specs, check_vma=False)
```

time: 346 us -> 110 us (0.32)
  blocking collectives: 143 us -> 0 us
  waiting for transfers between devices: 105 us -> 0 us
  Pallas kernels: 0 us -> 81.1 us
  matrix products: 64 us -> 23.5 us
  between operations: 16.6 us -> 1.33 us
  other arithmetic: 12.6 us -> 0 us
    reduce_scatter x4 -> x0, waiting for transfers between devices: 105 us -> none  [the longest x1 54.3 us: body(): lax.psum_scatter(total + router_grad[:, None] * router_weight, 'seq', sca...]
    all_gather x5 -> x0, blocking collectives: 90.7 us -> none  [the longest x1 33 us: body(): lax.all_gather(upstream, 'seq', axis=0, tiled=True)]
    pallas_call x0 -> x1, Pallas kernels: none -> 81.1 us  [body(): pl.pallas_call(functools.partial(kernel, ns, nt, nc, nk), out_shape=[jax....]
    psum x3 -> x0, blocking collectives: 46.9 us -> none  [the longest x1 35.6 us: body(): lax.psum((gain_part, router_part, live_counts[0].astype(jnp.float32)), 's...]
    dot_general x10 -> x3, matrix products: 64 us -> 23.5 us  [the longest x1 10.2 us: body(): grad_up = jnp.einsum('pd,pf->df', normed, d_up, preferred_element_type=f32)]
    unnamed x1 -> x0, blocking collectives: 5.73 us -> none
    convert_element_type x5 -> x0, other arithmetic: 4.73 us -> none  [the longest x2 3.16 us: body(): grad_out.astype(jnp.float32).at[slot_tokens].add(d_picked)]
  transfers between devices with their start and end apart: 4 -> 0, of which waited for: 3 -> 0; matrix products, arithmetic and copies ran while one was open for 5% -> 0% of each run, Pallas kernels for 0% -> 0%
where the time goes in v1:
time: 110 us
  Pallas kernels  81.1 us (74%)
  matrix products  23.5 us (21%)
  local copies, waits for them, and re-layouts  3.6 us (3%)
  between operations  1.33 us (1%)
    pallas_call x1, Pallas kernels, body(): pl.pallas_call(functools.partial(kernel, ns, nt, nc, nk), out_shape=[jax....  81.1 us
    dot_general x1, matrix products, body(): grad_up = jnp.einsum('pd,pf->df', normed, d_up, preferred_element_type=f32)  10.2 us
    dot_general x1, matrix products, body(): jnp.einsum('pd,pf->df', normed, d_gate, preferred_element_type=f32)  6.66 us
    dot_general x1, matrix products, body(): jnp.einsum('pf,pd->fd', weighted, upstream, preferred_element_type=f32)  6.65 us

profile of v1, /device:TPU:0, one launch (start us, length us, event | category | flops | bytes accessed | tf_op | source)
XLA Modules:
  0.0 109.5 jit_solution(12028278395141664835)
XLA Ops:
  1.3 1.3 %copy.15.tok_col = s32[16,1]{1,0:T(8,128)} copy(s32[16,1]{0,1:T(1,128)} %bitcast.23) | data formatting | bytes 128 | tf_op jit(solution)/shard_map/reshape | solution.py:562
  2.6 81.1 %shard_map.136 = (bf16[128,2048]{1,0:T(8,128)(2,1)}, f32[2,2048]{1,0:T(2,128)}, bf16[128,3072]{1,0:T(8,128)(2,1)}, bf16[128,3072]{1,0:T(8,128)(2,1)}, bf16[128,3...) custom-call(bf16[128,2048]{1,0:T(8,128)(2,1)} %hid.1, ...), custom_call_target="tpu_custom_call" | custom-call | tf_op jit(solution)/shard_map/pallas_call | solution.py:493
  83.7 0.0 copy-start.1
  83.7 0.0 copy-start.4
  83.7 0.0 copy-start.5
  83.8 1.4 %fusion = (f32[1,2048]{1,0:T(1,128)}, f32[1,2048]{1,0:T(1,128)}) fusion(f32[2,2048]{1,0:T(2,128)} %get-tuple-element.21), kind=kLoop, calls=%fused_computation.3 | loop fusion | bytes 32768 | tf_op jit(solution)/shard_map/slice | solution.py:581
  85.2 10.2 %multiply_convert_fusion.1 = bf16[2048,3072]{1,0:T(8,128)(2,1)} fusion(f32[]{:T(128)} %bitcast.20, bf16[128,2048]{1,0:T(8,128)(2,1)} %get-tuple-element.16, bf16[128,3072]{1,0:T(8,128)(2,1)} %get-tuple-element.18), kind=kOutput, calls=%fused_computation.1 | convolution fusion | flops 1623195648 | bytes 13893636 | tf_op jit(solution)/shard_map/pd,pf->df/dot_general | solution.py:573
  95.4 0.0 copy-done.1
  95.4 0.0 copy-done.4
  95.4 0.0 copy-done.5
  95.4 0.0 copy-start
  95.4 0.0 copy-start.2
  95.4 6.7 %multiply_convert_fusion = bf16[3072,2048]{1,0:T(8,128)(2,1)} fusion(f32[]{:T(128)S(1)} %bitcast.21, bf16[128,3072]{1,0:T(8,128)(2,1)S(1)} %copy-done.1, bf16[128,2048]{1,0:T(8,128)(2,1)S(1)} %copy-done.4), kind=kOutput, calls=%fused_computation | convolution fusion | flops 1623195648 | bytes 13893636 | tf_op jit(solution)/shard_map/pf,pd->fd/dot_general | solution.py:574
  102.1 0.0 copy-done
  102.1 0.0 copy-done.2
  102.1 0.0 copy-start.3
  102.1 6.7 %multiply_convert_fusion.2 = bf16[2048,3072]{1,0:T(8,128)(2,1)} fusion(f32[]{:T(128)S(1)} %bitcast.22, bf16[128,2048]{1,0:T(8,128)(2,1)S(1)} %copy-done, bf16[128,3072]{1,0:T(8,128)(2,1)S(1)} %copy-done.2), kind=kOutput, calls=%fused_computation.2 | convolution fusion | flops 1623195648 | bytes 13893636 | tf_op jit(solution)/shard_map/pd,pf->df/dot_general | solution.py:572
  108.7 0.0 copy-done.3
  108.7 0.8 copy.18
Async XLA Ops:
  83.7 11.6 %copy-start.1 = (bf16[128,3072]{1,0:T(8,128)(2,1)S(1)}, bf16[128,3072]{1,0:T(8,128)(2,1)}, u32[]{:S(2)}) copy-start(bf16[128,3072]{1,0:T(8,128)(2,1)} %get-tuple-element.19) | copy-start | bytes 2359300
  83.7 11.6 %copy-start.4 = (bf16[128,2048]{1,0:T(8,128)(2,1)S(1)}, bf16[128,2048]{1,0:T(8,128)(2,1)}, u32[]{:S(2)}) copy-start(bf16[128,2048]{1,0:T(8,128)(2,1)} %get-tuple-element.20) | copy-start | bytes 1572868
  83.7 11.6 %copy-start.5 = (f32[1,128]{1,0:T(1,128)S(1)}, f32[1,128]{1,0:T(1,128)}, u32[]{:S(2)}) copy-start(f32[1,128]{1,0:T(1,128)} %get-tuple-element.15) | copy-start | bytes 1540
  95.4 6.7 %copy-start = (bf16[128,2048]{1,0:T(8,128)(2,1)S(1)}, bf16[128,2048]{1,0:T(8,128)(2,1)}, u32[]{:S(2)}) copy-start(bf16[128,2048]{1,0:T(8,128)(2,1)} %get-tuple-element.16) | copy-start | bytes 1572868
  95.4 6.7 %copy-start.2 = (bf16[128,3072]{1,0:T(8,128)(2,1)S(1)}, bf16[128,3072]{1,0:T(8,128)(2,1)}, u32[]{:S(2)}) copy-start(bf16[128,3072]{1,0:T(8,128)(2,1)} %get-tuple-element.17) | copy-start | bytes 2359300
  102.1 6.7 %copy-start.3 = (bf16[128,2048]{1,0:T(8,128)(2,1)S(1)}, bf16[128,2048]{1,0:T(8,128)(2,1)}, u32[]{:S(2)}) copy-start(bf16[128,2048]{1,0:T(8,128)(2,1)} %get-tuple-element.30) | copy-start | bytes 1572868

commit v2 on v1

--- a/solution.py
+++ b/solution.py
@@ -22,6 +22,60 @@
 
 def nt_dot(a, b):
     return lax.dot_general(a, b, (((1,), (1,)), ((), ())), preferred_element_type=f32)
+
+
+def tn_dot(a, b):
+    return lax.dot_general(a, b, (((0,), (0,)), ((), ())), preferred_element_type=f32)
+
+
+def outer_kernel(norm, dg, du, wt, ups, cs, o_gate, o_up, o_down):
+    scale = cs[0:1, 0:1]
+
+    def fill(out, left, right):
+        size = right.shape[1]
+        piece = size // pick_chunks(size, (6, 4, 3, 2))
+        for n in range(0, size, piece):
+            out[:, n : n + piece] = (tn_dot(left, right[:, n : n + piece]) * scale).astype(bf16)
+
+    fill(o_gate, norm[...], dg)
+    fill(o_up, norm[...], du)
+    fill(o_down, wt[...], ups)
+
+
+def outer_products(normed, d_gate, d_up, weighted, upstream, scale):
+    rows, width = normed.shape
+    hidden = d_gate.shape[1]
+    steps = next(n for n in (8, 4, 2, 1) if width % (n * 128) == 0 and hidden % (n * 128) == 0)
+    tw, th = width // steps, hidden // steps
+
+    def whole(shape):
+        return pl.BlockSpec(shape, lambda i: (0, 0))
+
+    return pl.pallas_call(
+        outer_kernel,
+        grid=(steps,),
+        out_shape=[
+            jax.ShapeDtypeStruct((width, hidden), bf16),
+            jax.ShapeDtypeStruct((width, hidden), bf16),
+            jax.ShapeDtypeStruct((hidden, width), bf16),
+        ],
+        in_specs=[
+            pl.BlockSpec((rows, tw), lambda i: (0, i)),
+            whole((rows, hidden)),
+            whole((rows, hidden)),
+            pl.BlockSpec((rows, th), lambda i: (0, i)),
+            whole((rows, width)),
+            whole((1, 128)),
+        ],
+        out_specs=[
+            pl.BlockSpec((tw, hidden), lambda i: (i, 0)),
+            pl.BlockSpec((tw, hidden), lambda i: (i, 0)),
+            pl.BlockSpec((th, width), lambda i: (i, 0)),
+        ],
+        compiler_params=pltpu.CompilerParams(
+            dimension_semantics=("arbitrary",), vmem_limit_bytes=67_043_328
+        ),
+    )(normed, d_gate, d_up, weighted, upstream, scale)
 
 
 def kernel(
@@ -568,18 +622,10 @@
         up_weight,
         down_weight,
     )
-    count_scale = scale[0, 0]
-    grad_gate = jnp.einsum("pd,pf->df", normed, d_gate, preferred_element_type=f32)
-    grad_up = jnp.einsum("pd,pf->df", normed, d_up, preferred_element_type=f32)
-    grad_down = jnp.einsum("pf,pd->fd", weighted, upstream, preferred_element_type=f32)
-    return (
-        grad_in,
-        (count_scale * grad_gate).astype(bf16),
-        (count_scale * grad_up).astype(bf16),
-        (count_scale * grad_down).astype(bf16),
-        small[0],
-        small[1],
+    grad_gate, grad_up, grad_down = outer_products(
+        normed, d_gate, d_up, weighted, upstream, scale
     )
+    return (grad_in, grad_gate, grad_up, grad_down, small[0], small[1])
 
 
 def solution(mesh):

time: 110 us -> 102 us (0.927)
  matrix products: 23.5 us -> 0 us
  Pallas kernels: 81.1 us -> 95.6 us
    dot_general x3 -> x0, matrix products: 23.5 us -> none  [the longest x1 10.2 us: body(): grad_up = jnp.einsum('pd,pf->df', normed, d_up, preferred_element_type=f32)]
    pallas_call x0 -> x1, Pallas kernels: none -> 14.5 us  [outer_products(): pl.pallas_call(outer_kernel, grid=(steps,), out_shape=[jax.ShapeDtypeStru...]
where the time goes in v2:
time: 102 us; the launch traced here: 101 us
  Pallas kernels  95.6 us (94%)
  local copies, waits for them, and re-layouts  4.62 us (5%)
  between operations  1.29 us (1%)
    pallas_call x1, Pallas kernels, body(): pl.pallas_call(functools.partial(kernel, ns, nt, nc, nk), out_shape=[jax....  81.1 us
    pallas_call x1, Pallas kernels, outer_products(): pl.pallas_call(outer_kernel, grid=(steps,), out_shape=[jax.ShapeDtypeStru...  14.5 us

profile of v2, /device:TPU:0, one launch (start us, length us, event | category | flops | bytes accessed | tf_op | source)
XLA Modules:
  0.0 101.5 jit_solution(9535495646427675910)
XLA Ops:
  1.3 1.3 %copy.15.tok_col = s32[16,1]{1,0:T(8,128)} copy(s32[16,1]{0,1:T(1,128)} %bitcast.12) | data formatting | bytes 128 | tf_op jit(solution)/shard_map/reshape | solution.py:616
  2.6 81.1 %shard_map.136 = (bf16[128,2048]{1,0:T(8,128)(2,1)}, f32[2,2048]{1,0:T(2,128)}, bf16[128,3072]{1,0:T(8,128)(2,1)}, bf16[128,3072]{1,0:T(8,128)(2,1)}, bf16[128,3...) custom-call(bf16[128,2048]{1,0:T(8,128)(2,1)} %hid.1, ...), custom_call_target="tpu_custom_call" | custom-call | tf_op jit(solution)/shard_map/pallas_call | solution.py:547
  83.7 1.4 %fusion = (f32[1,2048]{1,0:T(1,128)}, f32[1,2048]{1,0:T(1,128)}) fusion(f32[2,2048]{1,0:T(2,128)} %get-tuple-element.27), kind=kLoop, calls=%fused_computation | loop fusion | bytes 32768 | tf_op jit(solution)/shard_map/slice | solution.py:628
  85.1 14.5 %shard_map.137 = (bf16[2048,3072]{1,0:T(8,128)(2,1)}, bf16[2048,3072]{1,0:T(8,128)(2,1)}, bf16[3072,2048]{1,0:T(8,128)(2,1)}) custom-call(bf16[128,2048]{1,0:T(8,128)(2,1)} %get-tuple-element.18.norm, bf16[128,3072]{1,0:T(8,128)(2,1)} %get-tuple-element.19.dg, bf16[128,3072]{1,0:T(8,128)(2,1)} %get-tuple-element.20.du, ...), custom_call_target="tpu_custom_call" | custom-call | tf_op jit(solution)/shard_map/pallas_call | solution.py:54
  99.6 1.9 %copy.18 = bf16[128,2048]{1,0:T(8,128)(2,1)} copy(bf16[128,2048]{1,0:T(8,128)(2,1)} %get-tuple-element.36) | data formatting | bytes 1048576
